TPU v7x, 128 devices: a whole 4x4x4 slice. The times are simulated.
128 devices in a mesh: outer: 8 (over z, y_lo), inner: 4 (over x_lo, core), heads: 4 (over y_hi, x_hi).
Axes of the slice: x: 4 (x_hi: 2, x_lo: 2; x = x_hi * 2 + x_lo), y: 4 (y_hi: 2, y_lo: 2; y = y_hi * 2 + y_lo), z: 4, core: 2. Of those that a mesh axis runs over, the one named last changes fastest.
Arguments:
- raw_keys: bfloat16 [32, 16384, 8, 128], P(None, ('outer', 'inner'), 'heads'), may hold values from -6 to 6
- raw_values: bfloat16 [32, 16384, 8, 128], P(None, ('outer', 'inner'), 'heads'), may hold values from -6 to 6
- turn_angle: float32 [16384, 64], replicated, may hold values from -3.140625 to 3.140625
Outputs:
- stored_keys: bfloat16 [32, 16384, 8, 128], P(('outer', 'inner'), None, 'heads')
- stored_values: bfloat16 [32, 16384, 8, 128], P(('outer', 'inner'), None, 'heads')
- page_high: bfloat16 [32, 256, 8, 128], P(('outer', 'inner'), None, 'heads')
- page_low: bfloat16 [32, 256, 8, 128], P(('outer', 'inner'), None, 'heads')
All inputs are finite; a program needn't handle non-finite values.
Results may differ from a plain program's by a relative error of at most 0.001.
Values may be sent and summed in bfloat16 or wider, within the bound.
A program may use at most 128 MiB of HBM per device.

v0:
```python
import jax
import jax.numpy as jnp
from jax import lax
from jax.sharding import PartitionSpec as P

PAGE = 64


def turn_pairs(vectors, angle):
    half = vectors.shape[-1] // 2
    cosine, sine = (jnp.cos(angle)[None, :, None, :], jnp.sin(angle)[None, :, None, :])
    first, second = (vectors[..., :half], vectors[..., half:])
    return jnp.concatenate(
        [first * cosine - second * sine, second * cosine + first * sine], axis=-1
    )


def prepare_keys(plain_keys, angle):
    wide_keys = plain_keys.astype(jnp.float32)
    return turn_pairs(wide_keys, angle)


def per_device(raw_keys, raw_values, turn_angle):
    my_angles = lax.dynamic_slice_in_dim(
        turn_angle, lax.axis_index(("outer", "inner")) * raw_keys.shape[1], raw_keys.shape[1]
    )
    sent_keys = prepare_keys(raw_keys, my_angles).astype(jnp.bfloat16)
    moved_keys, stored_values = (
        lax.all_to_all(sent_keys, ("outer", "inner"), split_axis=0, concat_axis=1, tiled=True),
        lax.all_to_all(raw_values, ("outer", "inner"), split_axis=0, concat_axis=1, tiled=True),
    )
    page_view = moved_keys.reshape(
        moved_keys.shape[0], -1, PAGE, moved_keys.shape[2], moved_keys.shape[3]
    )
    page_high = jnp.max(page_view, axis=2)
    page_low = jnp.min(page_view, axis=2)
    return (moved_keys, stored_values, page_high, page_low)


def solution(mesh):
    in_specs = (
        P(None, ("outer", "inner"), "heads", None),
        P(None, ("outer", "inner"), "heads", None),
        P(),
    )
    out_specs = (
        P(("outer", "inner"), None, "heads", None),
        P(("outer", "inner"), None, "heads", None),
        P(("outer", "inner"), None, "heads", None),
        P(("outer", "inner"), None, "heads", None),
    )
    return jax.shard_map(
        per_device, mesh=mesh, in_specs=in_specs, out_specs=out_specs, check_vma=False
    )
```

profile of v0, /device:TPU:1, one launch (start us, length us, event | category | flops | bytes accessed | tf_op | source)
XLA Modules:
  0.0 289.4 jit_solution(14165320990932599667)
XLA Ops:
  0.6 1.4 dynamic-slice_cosine_fusion
  2.0 0.1 copy.7
  2.1 0.1 copy.8
  2.3 9.1 %convert_element_type.4 = f32[32,512,2,128]{3,2,1,0:T(2,128)} convert(bf16[32,512,2,128]{3,2,1,0:T(2,128)(2,1)} %param.3) | non-fusion elementwise | flops 4194304 | bytes 25165824 | tf_op jit(solution)/shard_map/convert_element_type | solution.py:19
  11.4 24.5 %subtract_convert_fusion = (bf16[32,512,2,64]{3,2,1,0:T(2,128)(2,1)S(1)}, bf16[32,512,2,64]{3,2,1,0:T(2,128)(2,1)}) fusion(f32[32,512,2,128]{3,2,1,0:T(2,128)} %convert_element_type.4, f32[512,64]{1,0:T(8,128)S(1)} %copy.8, f32[512,64]{1,0:T(8,128)S(1)} %copy.7), kind=kLoop, calls=%fused_computation.1 | loop fusion | flops 16777216 | bytes 25427968 | tf_op jit(solution)/shard_map/convert
  35.9 24.1 %pad_maximum_fusion = bf16[32,512,2,128]{3,2,1,0:T(2,128)(2,1)S(1)} fusion(bf16[32,512,2,64]{3,2,1,0:T(2,128)(2,1)} %get-tuple-element.7, bf16[32,512,2,64]{3,2,1,0:T(2,128)(2,1)S(1)} %get-tuple-element.6), kind=kLoop, calls=%fused_computation.2 | loop fusion | flops 16777216 | bytes 16777216 | tf_op jit(solution)/shard_map/concatenate | solution.py:13
  60.0 104.2 %all_to_all.24 = bf16[32,512,2,128]{3,2,1,0:T(2,128)(2,1)} all-to-all(bf16[32,512,2,128]{3,2,1,0:T(2,128)(2,1)S(1)} %pad_maximum_fusion), channel_id=1, replica_groups=mesh['outer'=8,'inner'=4,'heads'=4] {'outer','inner'}, dimensions={0} | all-to-all | bytes 16777216 | tf_op jit(solution)/shard_map/all_to_all | solution.py:29
  164.1 5.5 %all-to-all-start.1 = ((bf16[32,512,2,128]{3,2,1,0:T(2,128)(2,1)}), bf16[32,512,2,128]{3,2,1,0:T(2,128)(2,1)}, u32[]{:S(2)}, u32[]{:S(2)}) async-start(bf16[32,512,2,128]{3,2,1,0:T(2,128)(2,1)} %param.4), calls=%async_computation.1 | async-start | bytes 16777216 | tf_op jit(solution)/shard_map/all_to_all | solution.py:30
  169.7 13.2 %fusion = (bf16[256,2,128]{2,1,0:T(2,128)(2,1)}, bf16[256,2,128]{2,1,0:T(2,128)(2,1)}) fusion(bf16[1,256,64,2,128]{4,3,2,1,0:T(2,128)(2,1)} %bitcast.5), kind=kLoop, calls=%fused_computation.5 | loop fusion | flops 8257536 | bytes 8650752 | tf_op jit(solution)/shard_map/reduce_min | solution.py:36
  182.9 90.6 %all-to-all-done.1 = bf16[32,512,2,128]{3,2,1,0:T(2,128)(2,1)} async-done(((bf16[32,512,2,128]{3,2,1,0:T(2,128)(2,1)}), bf16[32,512,2,128]{3,2,1,0:T(2,128)(2,1)}, u32[]{:S(2)}, u32[]{:S(2)}) %all-to-all-start.1) | async-done | bytes 8388640 | tf_op jit(solution)/shard_map/all_to_all | solution.py:30
  273.5 8.0 %copy.11 = bf16[1,16384,2,128]{3,2,1,0:T(2,128)(2,1)} copy(bf16[1,16384,2,128]{3,2,1,0:T(2,128)(2,1)} %bitcast.6) | data formatting | bytes 16777216
  281.5 8.0 %copy.12 = bf16[1,16384,2,128]{3,2,1,0:T(2,128)(2,1)} copy(bf16[1,16384,2,128]{3,2,1,0:T(2,128)(2,1)} %bitcast.1) | data formatting | bytes 16777216
Async XLA Ops:
  164.1 109.4 %all-to-all-start.1 = ((bf16[32,512,2,128]{3,2,1,0:T(2,128)(2,1)}), bf16[32,512,2,128]{3,2,1,0:T(2,128)(2,1)}, u32[]{:S(2)}, u32[]{:S(2)}) async-start(bf16[32,512,2,128]{3,2,1,0:T(2,128)(2,1)} %param.4), calls=%async_computation.1 | async-start | bytes 16777216 | tf_op jit(solution)/shard_map/all_to_all | solution.py:30
where the time goes:
time: 290 us; the launch traced here: 289 us
  blocking collectives  104 us (36%)
  waiting for transfers between devices  90.6 us (31%)
  other arithmetic  70.9 us (24%)
  local copies, waits for them, and re-layouts  17.6 us (6%)
  starting transfers between devices  5.53 us (2%)
    all_to_all x1, blocking collectives, per_device(): lax.all_to_all(sent_keys, ('outer', 'inner'), split_axis=0, concat_axis=1...  104 us
    all_to_all x1, waiting for transfers between devices, per_device(): lax.all_to_all(raw_values, ('outer', 'inner'), split_axis=0, concat_axis=...  90.6 us
    another operation x1, other arithmetic  24.5 us
    concatenate x1, other arithmetic, turn_pairs(): jnp.concatenate([first * cosine - second * sine, second * cosine + first...  24.1 us
    unnamed x2, local copies, waits for them, and re-layouts  15.9 us
    reduce_min x1, other arithmetic, per_device(): page_low = jnp.min(page_view, axis=2)  13.2 us
    convert_element_type x1, other arithmetic, prepare_keys(): wide_keys = plain_keys.astype(jnp.float32)  9.09 us
  transfers between devices with their start and end apart: 1, of which 1 were waited for; matrix products, arithmetic and copies ran while one was open for 5% of the time, Pallas kernels for 0%

commit v1 on v0

v1 whole, which is shorter than its diff:
```python
import jax
import jax.numpy as jnp
from jax import lax
from jax.experimental import pallas as pl
from jax.experimental.pallas import tpu as pltpu
from jax.sharding import PartitionSpec as P

MESH = pl.DeviceIdType.MESH
PAGE = 64
BLOCK = 128

UP, DOWN, BOTH = 1, 3, 2
SLOTS = (
    ((BOTH, 1, 1),),
    ((BOTH, 0, 1), (0, 1, 0)),
    ((BOTH, 1, 0), (0, 0, 1)),
    ((BOTH, 0, 0), (0, 1, 1)),
    ((UP, 1, 1), (DOWN, 0, 0)),
    ((DOWN, 1, 1), (UP, 0, 0)),
    ((UP, 0, 1), (DOWN, 1, 0)),
    ((UP, 1, 0), (DOWN, 0, 1)),
)
ORDER = tuple((*way, core) for slot in SLOTS for core in (0, 1) for way in slot) + ((0, 0, 0, 1),)


def position():
    outer, inner = lax.axis_index("outer"), lax.axis_index("inner")
    return outer // 2, outer % 2, inner // 2, inner % 2


def partner(step):
    z, y, x, core = position()
    return (
        ((z + step[0]) % 4) * 2 + (y + step[1]) % 2,
        ((x + step[2]) % 2) * 2 + (core + step[3]) % 2,
    )


def exchange_kernel(
    keys, values, angle, got_keys, got_values,
    turned, inbox, angles, cosines, sines,
    keys_sent, keys_came, values_sent, values_came, inbox_came, own_came,
):
    parts, rows, size = keys.shape
    heads = 2
    span = rows // heads
    z, y, x, core = position()
    me = (z * 2 + y) * 4 + x * 2 + core

    barrier = pltpu.get_barrier_semaphore()
    for step in ORDER:
        outer, inner = partner(step)
        pl.semaphore_signal(barrier, inc=1, device_id={"outer": outer, "inner": inner}, device_id_type=MESH)
    pl.semaphore_wait(barrier, len(ORDER))

    def send(source, target, sent, came, n):
        outer, inner = partner(ORDER[n])
        return pltpu.make_async_remote_copy(
            src_ref=source.at[outer * 4 + inner],
            dst_ref=target.at[me],
            send_sem=sent.at[n],
            recv_sem=came.at[n],
            device_id={"outer": outer, "inner": inner},
            device_id_type=MESH,
        )

    for n in range(len(ORDER)):
        send(values, got_values, values_sent, values_came, n).start()
    own_values = pltpu.make_async_copy(values.at[me], got_values.at[me], own_came.at[0])
    own_values.start()

    own_angles = pltpu.make_async_copy(
        angle.at[:, pl.ds(pl.multiple_of(me * span, span), span)], angles, own_came.at[1]
    )
    own_angles.start()

    def fetch(i, slot):
        return pltpu.make_async_copy(keys.at[lax.rem(me + 1 + i, parts)], inbox.at[slot], inbox_came.at[slot])

    fetch(0, 0).start()
    own_angles.wait()
    cosine, sine = jnp.cos(angles[...]), jnp.sin(angles[...])
    cosine = jnp.concatenate([cosine, cosine], axis=0).T
    sine = jnp.concatenate([-sine, sine], axis=0).T
    for head in range(heads):
        cosines[pl.ds(head, span, stride=heads), :] = cosine
        sines[pl.ds(head, span, stride=heads), :] = sine

    def turn(slot, target, at):
        def block(b, _):
            here = pl.ds(pl.multiple_of(b * BLOCK, BLOCK), BLOCK)
            wide = inbox[slot, here, :].astype(jnp.float32)
            other = pltpu.roll(wide, size // 2, 1)
            target[at, here, :] = (wide * cosines[here, :] + other * sines[here, :]).astype(jnp.bfloat16)
            return 0

        lax.fori_loop(0, rows // BLOCK, block, 0)

    def chunk(i, _):
        slot = lax.rem(i, 2)
        fetch(i + 1, 1 - slot).start()
        fetch(i, slot).wait()
        turn(slot, turned, lax.rem(me + 1 + i, parts))
        return 0

    lax.fori_loop(0, parts - 1, chunk, 0)
    last = (parts - 1) % 2
    fetch(parts - 1, last).wait()
    turn(last, got_keys, me)

    for n in range(len(ORDER)):
        send(turned, got_keys, keys_sent, keys_came, n).start()
    own_values.wait()
    for n in range(len(ORDER)):
        send(values, got_values, values_sent, values_came, n).wait()
    for n in range(len(ORDER)):
        send(turned, got_keys, keys_sent, keys_came, n).wait()


def store_kernel(got_keys, got_values, keys, values, high, low, highs, lows, flat, stored):
    parts, rows, size = got_keys.shape
    heads = 2
    page = PAGE * heads
    pages = rows // page
    tile = 16
    store_keys = pltpu.make_async_copy(got_keys, keys, stored.at[0])
    store_values = pltpu.make_async_copy(got_values, values, stored.at[1])
    store_keys.start()
    store_values.start()

    def part(s, _):
        for p in range(pages):
            block = [got_keys[s, pl.ds(p * page + t * tile, tile), :] for t in range(page // tile)]
            top, bottom = block[0], block[0]
            for piece in block[1:]:
                top, bottom = jnp.maximum(top, piece), jnp.minimum(bottom, piece)
            here = pl.ds(pl.multiple_of((s * pages + p) * tile, tile), tile)
            highs[here, :] = top.astype(jnp.float32)
            lows[here, :] = bottom.astype(jnp.float32)
        return 0

    lax.fori_loop(0, parts, part, 0)
    count = parts * pages
    for partial, pick, out in ((highs, jnp.maximum, high), (lows, jnp.minimum, low)):
        for head in range(heads):
            best = partial[pl.ds(head, count, stride=tile), :]
            for row in range(heads + head, tile, heads):
                best = pick(best, partial[pl.ds(row, count, stride=tile), :])
            flat[pl.ds(head, count, stride=heads), :] = best
        out[...] = flat[...].astype(jnp.bfloat16)

    store_keys.wait()
    store_values.wait()


def per_device(raw_keys, raw_values, turn_angle):
    parts, span, heads, size = raw_keys.shape
    rows = span * heads
    count = parts * span // PAGE
    steps = len(ORDER)
    near, far = (pl.BlockSpec(memory_space=space) for space in (pltpu.VMEM, pl.ANY))
    cache = (parts, rows, size)
    dma = pltpu.SemaphoreType.DMA
    got_keys, got_values = pl.pallas_call(
        exchange_kernel,
        out_shape=[pltpu.VMEM(cache, jnp.bfloat16)] * 2,
        in_specs=[far] * 3,
        out_specs=[near] * 2,
        scratch_shapes=[
            pltpu.VMEM(cache, jnp.bfloat16),
            pltpu.VMEM((2, rows, size), jnp.bfloat16),
            pltpu.VMEM((turn_angle.shape[1], span), jnp.float32),
            pltpu.VMEM((rows, size), jnp.float32),
            pltpu.VMEM((rows, size), jnp.float32),
            dma((steps,)), dma((steps,)), dma((steps,)), dma((steps,)), dma((2,)), dma((2,)),
        ],
        compiler_params=pltpu.CompilerParams(
            collective_id=0, has_side_effects=True, vmem_limit_bytes=40 * 1024 * 1024
        ),
        name="exchange",
    )(raw_keys.reshape(cache), raw_values.reshape(cache), turn_angle.T)
    keys, values, high, low = pl.pallas_call(
        store_kernel,
        out_shape=[jax.ShapeDtypeStruct(cache, jnp.bfloat16)] * 2
        + [jax.ShapeDtypeStruct((count * heads, size), jnp.bfloat16)] * 2,
        in_specs=[near] * 2,
        out_specs=[far] * 2 + [near] * 2,
        scratch_shapes=[
            pltpu.VMEM((count * 16, size), jnp.float32),
            pltpu.VMEM((count * 16, size), jnp.float32),
            pltpu.VMEM((count * heads, size), jnp.float32),
            dma((2,)),
        ],
        compiler_params=pltpu.CompilerParams(vmem_limit_bytes=24 * 1024 * 1024),
        name="store",
    )(got_keys, got_values)
    whole, bounds = (1, parts * span, heads, size), (1, count, heads, size)
    return keys.reshape(whole), values.reshape(whole), high.reshape(bounds), low.reshape(bounds)


def solution(mesh):
    cut = P(None, ("outer", "inner"), "heads", None)
    kept = P(("outer", "inner"), None, "heads", None)
    return jax.shard_map(
        per_device, mesh=mesh, in_specs=(cut, cut, P()), out_specs=(kept,) * 4, check_vma=False
    )
```

time: 290 us -> 200 us (0.69)
  Pallas kernels: 0 us -> 199 us
  blocking collectives: 104 us -> 0 us
  waiting for transfers between devices: 90.6 us -> 0 us
  other arithmetic: 70.9 us -> 0 us
  local copies, waits for them, and re-layouts: 17.6 us -> 0 us
  starting transfers between devices: 5.53 us -> 0 us
    pallas_call x0 -> x2, Pallas kernels: none -> 199 us  [the longest x1 192 us: per_device(): pl.pallas_call(exchange_kernel, out_shape=[pltpu.VMEM(cache, jnp.bfloat16...]
    all_to_all x1 -> x0, blocking collectives: 104 us -> none  [per_device(): lax.all_to_all(sent_keys, ('outer', 'inner'), split_axis=0, concat_axis=1...]
    all_to_all x1 -> x0, waiting for transfers between devices: 90.6 us -> none  [per_device(): lax.all_to_all(raw_values, ('outer', 'inner'), split_axis=0, concat_axis=...]
    another operation x1 -> x0, other arithmetic: 24.5 us -> none
    concatenate x1 -> x0, other arithmetic: 24.1 us -> none  [turn_pairs(): jnp.concatenate([first * cosine - second * sine, second * cosine + first...]
    unnamed x2 -> x0, local copies, waits for them, and re-layouts: 15.9 us -> none
    reduce_min x1 -> x0, other arithmetic: 13.2 us -> none  [per_device(): page_low = jnp.min(page_view, axis=2)]
    convert_element_type x1 -> x0, other arithmetic: 9.09 us -> none  [prepare_keys(): wide_keys = plain_keys.astype(jnp.float32)]
  transfers between devices with their start and end apart: 1 -> 0, of which waited for: 1 -> 0; matrix products, arithmetic and copies ran while one was open for 5% -> 0% of each run, Pallas kernels for 0% -> 0%
where the time goes in v1:
time: 200 us; the launch traced here: 199 us
  Pallas kernels  199 us (100%)
    pallas_call x1, Pallas kernels, per_device(): pl.pallas_call(exchange_kernel, out_shape=[pltpu.VMEM(cache, jnp.bfloat16...  192 us
    pallas_call x1, Pallas kernels, per_device(): pl.pallas_call(store_kernel, out_shape=[jax.ShapeDtypeStruct(cache, jnp.b...  6.87 us

profile of v1, /device:TPU:1, one launch (start us, length us, event | category | flops | bytes accessed | tf_op | source)
XLA Modules:
  0.0 199.2 jit_solution(5499408475327075101)
XLA Ops:
  0.6 191.7 %exchange.1 = (bf16[32,1024,128]{2,1,0:T(8,128)(2,1)S(1)}, bf16[32,1024,128]{2,1,0:T(8,128)(2,1)S(1)}) custom-call(bf16[32,1024,128]{2,1,0:T(8,128)(2,1)} %bitcast.7, bf16[32,1024,128]{2,1,0:T(8,128)(2,1)} %bitcast.8, f32[64,16384]{1,0:T(8,128)} %bitcast.9), custom_call_target="tpu_custom_call" | custom-call | tf_op jit(solution)/shard_map/exchange/pallas_call | solution.py:164
  192.3 6.9 %store.1 = (bf16[32,1024,128]{2,1,0:T(8,128)(2,1)}, bf16[32,1024,128]{2,1,0:T(8,128)(2,1)}, bf16[512,128]{1,0:T(8,128)(2,1)}, bf16[512,128]{1,0:T(8,128)(2,1)}) custom-call(bf16[32,1024,128]{2,1,0:T(8,128)(2,1)S(1)} %get-tuple-element.10.got_keys, bf16[32,1024,128]{2,1,0:T(8,128)(2,1)S(1)} %get-tuple-element.11.got_values), custom_call_target="tpu_custom_call" | custom-call | tf_op jit(solution)/shard_map/store/pallas_call | solution.py:182

commit v2 on v1

--- a/solution.py
+++ b/solution.py
@@ -21,6 +21,8 @@
     ((UP, 1, 0), (DOWN, 0, 1)),
 )
 ORDER = tuple((*way, core) for slot in SLOTS for core in (0, 1) for way in slot) + ((0, 0, 0, 1),)
+STARTS = tuple(2 * sum(map(len, SLOTS[:s])) for s in range(len(SLOTS) + 1)) + (len(ORDER),)
+GROUPS = tuple(tuple(range(a, b)) for a, b in zip(STARTS, STARTS[1:]))
 
 
 def position():
@@ -38,8 +40,8 @@
 
 def exchange_kernel(
     keys, values, angle, got_keys, got_values,
-    turned, inbox, angles, cosines, sines,
-    keys_sent, keys_came, values_sent, values_came, inbox_came, own_came,
+    turned, angles, cosines, sines,
+    keys_sent, keys_came, values_sent, values_came, fetched, own_came,
 ):
     parts, rows, size = keys.shape
     heads = 2
@@ -51,7 +53,19 @@
     for step in ORDER:
         outer, inner = partner(step)
         pl.semaphore_signal(barrier, inc=1, device_id={"outer": outer, "inner": inner}, device_id_type=MESH)
-    pl.semaphore_wait(barrier, len(ORDER))
+
+    own_angles = pltpu.make_async_copy(
+        angle.at[:, pl.ds(pl.multiple_of(me * span, span), span)], angles, own_came.at[0]
+    )
+    own_keys = pltpu.make_async_copy(keys.at[me], got_keys.at[me], own_came.at[1])
+    own_values = pltpu.make_async_copy(values.at[me], got_values.at[me], own_came.at[2])
+
+    def where(n):
+        outer, inner = partner(ORDER[n])
+        return outer * 4 + inner
+
+    def fetch(n):
+        return pltpu.make_async_copy(keys.at[where(n)], turned.at[where(n)], fetched.at[n])
 
     def send(source, target, sent, came, n):
         outer, inner = partner(ORDER[n])
@@ -64,20 +78,22 @@
             device_id_type=MESH,
         )
 
+    def send_keys(n):
+        return send(turned, got_keys, keys_sent, keys_came, n)
+
+    def send_values(n):
+        return send(values, got_values, values_sent, values_came, n)
+
+    pl.semaphore_wait(barrier, len(ORDER))
+
+    for n in GROUPS[0]:
+        send_values(n).start()
+
+    own_angles.start()
     for n in range(len(ORDER)):
-        send(values, got_values, values_sent, values_came, n).start()
-    own_values = pltpu.make_async_copy(values.at[me], got_values.at[me], own_came.at[0])
+        fetch(n).start()
+    own_keys.start()
     own_values.start()
-
-    own_angles = pltpu.make_async_copy(
-        angle.at[:, pl.ds(pl.multiple_of(me * span, span), span)], angles, own_came.at[1]
-    )
-    own_angles.start()
-
-    def fetch(i, slot):
-        return pltpu.make_async_copy(keys.at[lax.rem(me + 1 + i, parts)], inbox.at[slot], inbox_came.at[slot])
-
-    fetch(0, 0).start()
     own_angles.wait()
     cosine, sine = jnp.cos(angles[...]), jnp.sin(angles[...])
     cosine = jnp.concatenate([cosine, cosine], axis=0).T
@@ -86,38 +102,42 @@
         cosines[pl.ds(head, span, stride=heads), :] = cosine
         sines[pl.ds(head, span, stride=heads), :] = sine
 
-    def turn(slot, target, at):
+    def turn(cache, at):
         def block(b, _):
             here = pl.ds(pl.multiple_of(b * BLOCK, BLOCK), BLOCK)
-            wide = inbox[slot, here, :].astype(jnp.float32)
+            wide = cache[at, here, :].astype(jnp.float32)
             other = pltpu.roll(wide, size // 2, 1)
-            target[at, here, :] = (wide * cosines[here, :] + other * sines[here, :]).astype(jnp.bfloat16)
+            cache[at, here, :] = (wide * cosines[here, :] + other * sines[here, :]).astype(jnp.bfloat16)
             return 0
 
         lax.fori_loop(0, rows // BLOCK, block, 0)
 
-    def chunk(i, _):
-        slot = lax.rem(i, 2)
-        fetch(i + 1, 1 - slot).start()
-        fetch(i, slot).wait()
-        turn(slot, turned, lax.rem(me + 1 + i, parts))
-        return 0
-
-    lax.fori_loop(0, parts - 1, chunk, 0)
-    last = (parts - 1) % 2
-    fetch(parts - 1, last).wait()
-    turn(last, got_keys, me)
-
-    for n in range(len(ORDER)):
-        send(turned, got_keys, keys_sent, keys_came, n).start()
+    def turn_group(group):
+        for n in group:
+            fetch(n).wait()
+            turn(turned, where(n))
+
+    for s, group in enumerate(GROUPS):
+        if s:
+            for n in group:
+                send_values(n).start()
+        if s == 0:
+            turn_group(group)
+        if s + 1 < len(GROUPS):
+            turn_group(GROUPS[s + 1])
+        else:
+            own_keys.wait()
+            turn(got_keys, me)
+        for n in group:
+            send_keys(n).start()
+
     own_values.wait()
     for n in range(len(ORDER)):
-        send(values, got_values, values_sent, values_came, n).wait()
-    for n in range(len(ORDER)):
-        send(turned, got_keys, keys_sent, keys_came, n).wait()
-
-
-def store_kernel(got_keys, got_values, keys, values, high, low, highs, lows, flat, stored):
+        send_values(n).wait()
+        send_keys(n).wait()
+
+
+def store_kernel(got_keys, got_values, keys, values, high, low, highs, lows, flat, bounds, stored):
     parts, rows, size = got_keys.shape
     heads = 2
     page = PAGE * heads
@@ -141,16 +161,20 @@
 
     lax.fori_loop(0, parts, part, 0)
     count = parts * pages
-    for partial, pick, out in ((highs, jnp.maximum, high), (lows, jnp.minimum, low)):
+    store_bounds = [
+        pltpu.make_async_copy(bounds.at[side], out, stored.at[2 + side]) for side, out in enumerate((high, low))
+    ]
+    for side, (partial, pick) in enumerate(((highs, jnp.maximum), (lows, jnp.minimum))):
         for head in range(heads):
             best = partial[pl.ds(head, count, stride=tile), :]
             for row in range(heads + head, tile, heads):
                 best = pick(best, partial[pl.ds(row, count, stride=tile), :])
             flat[pl.ds(head, count, stride=heads), :] = best
-        out[...] = flat[...].astype(jnp.bfloat16)
-
-    store_keys.wait()
-    store_values.wait()
+        bounds[side] = flat[...].astype(jnp.bfloat16)
+    for store in store_bounds:
+        store.start()
+    for store in (store_keys, store_values, *store_bounds):
+        store.wait()
 
 
 def per_device(raw_keys, raw_values, turn_angle):
@@ -168,11 +192,10 @@
         out_specs=[near] * 2,
         scratch_shapes=[
             pltpu.VMEM(cache, jnp.bfloat16),
-            pltpu.VMEM((2, rows, size), jnp.bfloat16),
             pltpu.VMEM((turn_angle.shape[1], span), jnp.float32),
             pltpu.VMEM((rows, size), jnp.float32),
             pltpu.VMEM((rows, size), jnp.float32),
-            dma((steps,)), dma((steps,)), dma((steps,)), dma((steps,)), dma((2,)), dma((2,)),
+            dma((steps,)), dma((steps,)), dma((steps,)), dma((steps,)), dma((steps,)), dma((3,)),
         ],
         compiler_params=pltpu.CompilerParams(
             collective_id=0, has_side_effects=True, vmem_limit_bytes=40 * 1024 * 1024
@@ -184,12 +207,13 @@
         out_shape=[jax.ShapeDtypeStruct(cache, jnp.bfloat16)] * 2
         + [jax.ShapeDtypeStruct((count * heads, size), jnp.bfloat16)] * 2,
         in_specs=[near] * 2,
-        out_specs=[far] * 2 + [near] * 2,
+        out_specs=[far] * 4,
         scratch_shapes=[
             pltpu.VMEM((count * 16, size), jnp.float32),
             pltpu.VMEM((count * 16, size), jnp.float32),
             pltpu.VMEM((count * heads, size), jnp.float32),
-            dma((2,)),
+            pltpu.VMEM((2, count * heads, size), jnp.bfloat16),
+            dma((4,)),
         ],
         compiler_params=pltpu.CompilerParams(vmem_limit_bytes=24 * 1024 * 1024),
         name="store",

time: 200 us -> 198 us (0.990)
  Pallas kernels: 199 us -> 197 us
where the time goes in v2:
time: 198 us
  Pallas kernels  197 us (99%)
    pallas_call x1, Pallas kernels, per_device(): pl.pallas_call(exchange_kernel, out_shape=[pltpu.VMEM(cache, jnp.bfloat16...  191 us
    pallas_call x1, Pallas kernels, per_device(): pl.pallas_call(store_kernel, out_shape=[jax.ShapeDtypeStruct(cache, jnp.b...  6.2 us

profile of v2, /device:TPU:1, one launch (start us, length us, event | category | flops | bytes accessed | tf_op | source)
XLA Modules:
  0.0 198.1 jit_solution(13936801125848744431)
XLA Ops:
  0.6 191.2 %exchange.1 = (bf16[32,1024,128]{2,1,0:T(8,128)(2,1)S(1)}, bf16[32,1024,128]{2,1,0:T(8,128)(2,1)S(1)}) custom-call(bf16[32,1024,128]{2,1,0:T(8,128)(2,1)} %bitcast.7, bf16[32,1024,128]{2,1,0:T(8,128)(2,1)} %bitcast.8, f32[64,16384]{1,0:T(8,128)} %bitcast.9), custom_call_target="tpu_custom_call" | custom-call | tf_op jit(solution)/shard_map/exchange/pallas_call | solution.py:188
  191.9 6.2 %store.1 = (bf16[32,1024,128]{2,1,0:T(8,128)(2,1)}, bf16[32,1024,128]{2,1,0:T(8,128)(2,1)}, bf16[512,128]{1,0:T(8,128)(2,1)}, bf16[512,128]{1,0:T(8,128)(2,1)}) custom-call(bf16[32,1024,128]{2,1,0:T(8,128)(2,1)S(1)} %get-tuple-element.10.got_keys, bf16[32,1024,128]{2,1,0:T(8,128)(2,1)S(1)} %get-tuple-element.11.got_values), custom_call_target="tpu_custom_call" | custom-call | tf_op jit(solution)/shard_map/store/pallas_call | solution.py:205

commit v3 on v2

--- a/solution.py
+++ b/solution.py
@@ -7,7 +7,7 @@
 
 MESH = pl.DeviceIdType.MESH
 PAGE = 64
-BLOCK = 128
+BLOCK = 256
 
 UP, DOWN, BOTH = 1, 3, 2
 SLOTS = (
@@ -41,7 +41,7 @@
 def exchange_kernel(
     keys, values, angle, got_keys, got_values,
     turned, angles, cosines, sines,
-    keys_sent, keys_came, values_sent, values_came, fetched, own_came,
+    keys_sent, keys_came, values_sent, values_came, own_came,
 ):
     parts, rows, size = keys.shape
     heads = 2
@@ -57,15 +57,9 @@
     own_angles = pltpu.make_async_copy(
         angle.at[:, pl.ds(pl.multiple_of(me * span, span), span)], angles, own_came.at[0]
     )
-    own_keys = pltpu.make_async_copy(keys.at[me], got_keys.at[me], own_came.at[1])
     own_values = pltpu.make_async_copy(values.at[me], got_values.at[me], own_came.at[2])
 
-    def where(n):
-        outer, inner = partner(ORDER[n])
-        return outer * 4 + inner
-
-    def fetch(n):
-        return pltpu.make_async_copy(keys.at[where(n)], turned.at[where(n)], fetched.at[n])
+    all_keys = pltpu.make_async_copy(keys, turned, own_came.at[1])
 
     def send(source, target, sent, came, n):
         outer, inner = partner(ORDER[n])
@@ -86,13 +80,11 @@
 
     pl.semaphore_wait(barrier, len(ORDER))
 
-    for n in GROUPS[0]:
+    for n in GROUPS[0] + GROUPS[1]:
         send_values(n).start()
 
     own_angles.start()
-    for n in range(len(ORDER)):
-        fetch(n).start()
-    own_keys.start()
+    all_keys.start()
     own_values.start()
     own_angles.wait()
     cosine, sine = jnp.cos(angles[...]), jnp.sin(angles[...])
@@ -102,32 +94,28 @@
         cosines[pl.ds(head, span, stride=heads), :] = cosine
         sines[pl.ds(head, span, stride=heads), :] = sine
 
-    def turn(cache, at):
+    def turn(source, target, at):
         def block(b, _):
             here = pl.ds(pl.multiple_of(b * BLOCK, BLOCK), BLOCK)
-            wide = cache[at, here, :].astype(jnp.float32)
+            wide = source[at, here, :].astype(jnp.float32)
             other = pltpu.roll(wide, size // 2, 1)
-            cache[at, here, :] = (wide * cosines[here, :] + other * sines[here, :]).astype(jnp.bfloat16)
+            target[at, here, :] = (wide * cosines[here, :] + other * sines[here, :]).astype(jnp.bfloat16)
             return 0
 
         lax.fori_loop(0, rows // BLOCK, block, 0)
 
-    def turn_group(group):
+    def turn_part(i, _):
+        turn(turned, turned, lax.rem(me + 1 + i, parts))
+        return 0
+
+    all_keys.wait()
+    lax.fori_loop(0, parts - 1, turn_part, 0)
+    turn(turned, got_keys, me)
+    for n in GROUPS[1] + GROUPS[0]:
+        send_keys(n).start()
+    for group in GROUPS[2:]:
         for n in group:
-            fetch(n).wait()
-            turn(turned, where(n))
-
-    for s, group in enumerate(GROUPS):
-        if s:
-            for n in group:
-                send_values(n).start()
-        if s == 0:
-            turn_group(group)
-        if s + 1 < len(GROUPS):
-            turn_group(GROUPS[s + 1])
-        else:
-            own_keys.wait()
-            turn(got_keys, me)
+            send_values(n).start()
         for n in group:
             send_keys(n).start()
 
@@ -143,10 +131,14 @@
     page = PAGE * heads
     pages = rows // page
     tile = 16
-    store_keys = pltpu.make_async_copy(got_keys, keys, stored.at[0])
-    store_values = pltpu.make_async_copy(got_values, values, stored.at[1])
-    store_keys.start()
-    store_values.start()
+    pieces = 8
+    stores = [
+        pltpu.make_async_copy(got.at[pl.ds(p, parts // pieces)], out.at[pl.ds(p, parts // pieces)], stored.at[side, i])
+        for i, p in enumerate(range(0, parts, parts // pieces))
+        for side, (got, out) in enumerate(((got_keys, keys), (got_values, values)))
+    ]
+    for store in stores:
+        store.start()
 
     def part(s, _):
         for p in range(pages):
@@ -162,7 +154,7 @@
     lax.fori_loop(0, parts, part, 0)
     count = parts * pages
     store_bounds = [
-        pltpu.make_async_copy(bounds.at[side], out, stored.at[2 + side]) for side, out in enumerate((high, low))
+        pltpu.make_async_copy(bounds.at[side], out, stored.at[side, pieces]) for side, out in enumerate((high, low))
     ]
     for side, (partial, pick) in enumerate(((highs, jnp.maximum), (lows, jnp.minimum))):
         for head in range(heads):
@@ -173,7 +165,7 @@
         bounds[side] = flat[...].astype(jnp.bfloat16)
     for store in store_bounds:
         store.start()
-    for store in (store_keys, store_values, *store_bounds):
+    for store in (*stores, *store_bounds):
         store.wait()
 
 
@@ -195,7 +187,7 @@
             pltpu.VMEM((turn_angle.shape[1], span), jnp.float32),
             pltpu.VMEM((rows, size), jnp.float32),
             pltpu.VMEM((rows, size), jnp.float32),
-            dma((steps,)), dma((steps,)), dma((steps,)), dma((steps,)), dma((steps,)), dma((3,)),
+            dma((steps,)), dma((steps,)), dma((steps,)), dma((steps,)), dma((3,)),
         ],
         compiler_params=pltpu.CompilerParams(
             collective_id=0, has_side_effects=True, vmem_limit_bytes=40 * 1024 * 1024
@@ -213,7 +205,7 @@
             pltpu.VMEM((count * 16, size), jnp.float32),
             pltpu.VMEM((count * heads, size), jnp.float32),
             pltpu.VMEM((2, count * heads, size), jnp.bfloat16),
-            dma((4,)),
+            dma((2, 9)),
         ],
         compiler_params=pltpu.CompilerParams(vmem_limit_bytes=24 * 1024 * 1024),
         name="store",

time: 198 us -> 198 us (level)
  no operation moved by 1% of the time
where the time goes in v3:
time: 198 us
  Pallas kernels  197 us (99%)
    pallas_call x1, Pallas kernels, per_device(): pl.pallas_call(exchange_kernel, out_shape=[pltpu.VMEM(cache, jnp.bfloat16...  191 us
    pallas_call x1, Pallas kernels, per_device(): pl.pallas_call(store_kernel, out_shape=[jax.ShapeDtypeStruct(cache, jnp.b...  6.02 us

profile of v3, /device:TPU:1, one launch (start us, length us, event | category | flops | bytes accessed | tf_op | source)
XLA Modules:
  0.0 197.6 jit_solution(12816460471832983220)
XLA Ops:
  0.6 190.9 %exchange.1 = (bf16[32,1024,128]{2,1,0:T(8,128)(2,1)S(1)}, bf16[32,1024,128]{2,1,0:T(8,128)(2,1)S(1)}) custom-call(bf16[32,1024,128]{2,1,0:T(8,128)(2,1)} %bitcast.7, bf16[32,1024,128]{2,1,0:T(8,128)(2,1)} %bitcast.8, f32[64,16384]{1,0:T(8,128)} %bitcast.9), custom_call_target="tpu_custom_call" | custom-call | tf_op jit(solution)/shard_map/exchange/pallas_call | solution.py:180
  191.5 6.0 %store.1 = (bf16[32,1024,128]{2,1,0:T(8,128)(2,1)}, bf16[32,1024,128]{2,1,0:T(8,128)(2,1)}, bf16[512,128]{1,0:T(8,128)(2,1)}, bf16[512,128]{1,0:T(8,128)(2,1)}) custom-call(bf16[32,1024,128]{2,1,0:T(8,128)(2,1)S(1)} %get-tuple-element.10.got_keys, bf16[32,1024,128]{2,1,0:T(8,128)(2,1)S(1)} %get-tuple-element.11.got_values), custom_call_target="tpu_custom_call" | custom-call | tf_op jit(solution)/shard_map/store/pallas_call | solution.py:197

commit v4 on v3

--- a/solution.py
+++ b/solution.py
@@ -40,8 +40,8 @@
 
 def exchange_kernel(
     keys, values, angle, got_keys, got_values,
-    turned, angles, cosines, sines,
-    keys_sent, keys_came, values_sent, values_came, own_came,
+    turned, first, angles, cosines, sines,
+    keys_sent, keys_came, values_sent, values_came, first_came, own_came,
 ):
     parts, rows, size = keys.shape
     heads = 2
@@ -49,6 +49,13 @@
     z, y, x, core = position()
     me = (z * 2 + y) * 4 + x * 2 + core
 
+    def fetch_first(n):
+        outer, inner = partner(ORDER[n])
+        return pltpu.make_async_copy(values.at[outer * 4 + inner], first.at[n], first_came.at[n])
+
+    for n in GROUPS[0]:
+        fetch_first(n).start()
+
     barrier = pltpu.get_barrier_semaphore()
     for step in ORDER:
         outer, inner = partner(step)
@@ -61,10 +68,10 @@
 
     all_keys = pltpu.make_async_copy(keys, turned, own_came.at[1])
 
-    def send(source, target, sent, came, n):
+    def send(source, target, sent, came, n, held=None):
         outer, inner = partner(ORDER[n])
         return pltpu.make_async_remote_copy(
-            src_ref=source.at[outer * 4 + inner],
+            src_ref=source.at[outer * 4 + inner] if held is None else held,
             dst_ref=target.at[me],
             send_sem=sent.at[n],
             recv_sem=came.at[n],
@@ -76,10 +83,12 @@
         return send(turned, got_keys, keys_sent, keys_came, n)
 
     def send_values(n):
-        return send(values, got_values, values_sent, values_came, n)
+        return send(values, got_values, values_sent, values_came, n, first.at[n] if n in GROUPS[0] else None)
 
     pl.semaphore_wait(barrier, len(ORDER))
 
+    for n in GROUPS[0]:
+        fetch_first(n).wait()
     for n in GROUPS[0] + GROUPS[1]:
         send_values(n).start()
 
@@ -184,10 +193,11 @@
         out_specs=[near] * 2,
         scratch_shapes=[
             pltpu.VMEM(cache, jnp.bfloat16),
+            pltpu.VMEM((len(GROUPS[0]), rows, size), jnp.bfloat16),
             pltpu.VMEM((turn_angle.shape[1], span), jnp.float32),
             pltpu.VMEM((rows, size), jnp.float32),
             pltpu.VMEM((rows, size), jnp.float32),
-            dma((steps,)), dma((steps,)), dma((steps,)), dma((steps,)), dma((3,)),
+            dma((steps,)), dma((steps,)), dma((steps,)), dma((steps,)), dma((len(GROUPS[0]),)), dma((3,)),
         ],
         compiler_params=pltpu.CompilerParams(
             collective_id=0, has_side_effects=True, vmem_limit_bytes=40 * 1024 * 1024

time: 198 us -> 198 us (level)
  no operation moved by 1% of the time
where the time goes in v4:
time: 198 us; the launch traced here: 197 us
  Pallas kernels  197 us (99%)
    pallas_call x1, Pallas kernels, per_device(): pl.pallas_call(exchange_kernel, out_shape=[pltpu.VMEM(cache, jnp.bfloat16...  191 us
    pallas_call x1, Pallas kernels, per_device(): pl.pallas_call(store_kernel, out_shape=[jax.ShapeDtypeStruct(cache, jnp.b...  6.02 us

profile of v4, /device:TPU:1, one launch (start us, length us, event | category | flops | bytes accessed | tf_op | source)
XLA Modules:
  0.0 197.4 jit_solution(4385666739332183995)
XLA Ops:
  0.6 190.8 %exchange.1 = (bf16[32,1024,128]{2,1,0:T(8,128)(2,1)S(1)}, bf16[32,1024,128]{2,1,0:T(8,128)(2,1)S(1)}) custom-call(bf16[32,1024,128]{2,1,0:T(8,128)(2,1)} %bitcast.7, bf16[32,1024,128]{2,1,0:T(8,128)(2,1)} %bitcast.8, f32[64,16384]{1,0:T(8,128)} %bitcast.9), custom_call_target="tpu_custom_call" | custom-call | tf_op jit(solution)/shard_map/exchange/pallas_call | solution.py:189
  191.4 6.0 %store.1 = (bf16[32,1024,128]{2,1,0:T(8,128)(2,1)}, bf16[32,1024,128]{2,1,0:T(8,128)(2,1)}, bf16[512,128]{1,0:T(8,128)(2,1)}, bf16[512,128]{1,0:T(8,128)(2,1)}) custom-call(bf16[32,1024,128]{2,1,0:T(8,128)(2,1)S(1)} %get-tuple-element.10.got_keys, bf16[32,1024,128]{2,1,0:T(8,128)(2,1)S(1)} %get-tuple-element.11.got_values), custom_call_target="tpu_custom_call" | custom-call | tf_op jit(solution)/shard_map/store/pallas_call | solution.py:207

commit v5 on v4

--- a/solution.py
+++ b/solution.py
@@ -27,15 +27,14 @@
 
 def position():
     outer, inner = lax.axis_index("outer"), lax.axis_index("inner")
-    return outer // 2, outer % 2, inner // 2, inner % 2
+    z, x = lax.div(outer, 2), lax.div(inner, 2)
+    return z, outer - 2 * z, x, inner - 2 * x
 
 
 def partner(step):
     z, y, x, core = position()
-    return (
-        ((z + step[0]) % 4) * 2 + (y + step[1]) % 2,
-        ((x + step[2]) % 2) * 2 + (core + step[3]) % 2,
-    )
+    flip = lambda bit, over: 1 - bit if over else bit
+    return lax.rem(z + step[0], 4) * 2 + flip(y, step[1]), flip(x, step[2]) * 2 + flip(core, step[3])
 
 
 def exchange_kernel(

time: 198 us -> 198 us (level)
  no operation moved by 1% of the time
where the time goes in v5:
time: 198 us; the launch traced here: 197 us
  Pallas kernels  197 us (99%)
    pallas_call x1, Pallas kernels, per_device(): pl.pallas_call(exchange_kernel, out_shape=[pltpu.VMEM(cache, jnp.bfloat16...  191 us
    pallas_call x1, Pallas kernels, per_device(): pl.pallas_call(store_kernel, out_shape=[jax.ShapeDtypeStruct(cache, jnp.b...  6.02 us

profile of v5, /device:TPU:1, one launch (start us, length us, event | category | flops | bytes accessed | tf_op | source)
XLA Modules:
  0.0 197.4 jit_solution(2249014022800545214)
XLA Ops:
  0.6 190.7 %exchange.1 = (bf16[32,1024,128]{2,1,0:T(8,128)(2,1)S(1)}, bf16[32,1024,128]{2,1,0:T(8,128)(2,1)S(1)}) custom-call(bf16[32,1024,128]{2,1,0:T(8,128)(2,1)} %bitcast.7, bf16[32,1024,128]{2,1,0:T(8,128)(2,1)} %bitcast.8, f32[64,16384]{1,0:T(8,128)} %bitcast.9), custom_call_target="tpu_custom_call" | custom-call | tf_op jit(solution)/shard_map/exchange/pallas_call | solution.py:188
  191.4 6.0 %store.1 = (bf16[32,1024,128]{2,1,0:T(8,128)(2,1)}, bf16[32,1024,128]{2,1,0:T(8,128)(2,1)}, bf16[512,128]{1,0:T(8,128)(2,1)}, bf16[512,128]{1,0:T(8,128)(2,1)}) custom-call(bf16[32,1024,128]{2,1,0:T(8,128)(2,1)S(1)} %get-tuple-element.10.got_keys, bf16[32,1024,128]{2,1,0:T(8,128)(2,1)S(1)} %get-tuple-element.11.got_values), custom_call_target="tpu_custom_call" | custom-call | tf_op jit(solution)/shard_map/store/pallas_call | solution.py:206
